TPU v7x, 32 devices: a whole 2x2x4 slice. The times are simulated.
32 devices in a mesh: dp: 4 (over y, x), expert: 4 (over z), tensor: 2 (over core).
Axes of the slice: x: 2, y: 2, z: 4, core: 2. Of those that a mesh axis runs over, the one named last changes fastest.
Arguments:
- tokens: bfloat16 [2048, 2560], P(('dp', 'expert')), may hold values from -6 to 6
- norm_gain: float32 [2560], replicated, may hold values from 0.5 to 1.5
- expert_ids: int32 [2048, 6], P(('dp', 'expert')), may hold values from 0 to 31, all different within a row; in each aligned block of 128 rows (0 to 127, 128 to 255, ...) at most 48 rows name the same one
- route_weights: int32 [2048, 6], P(('dp', 'expert')), may hold values from 1 to 64
- w_gate: bfloat16 [32, 2560, 768], P('expert', None, 'tensor'), may hold values from -0.125 to 0.125
- w_up: bfloat16 [32, 2560, 768], P('expert', None, 'tensor'), may hold values from -0.125 to 0.125
- w_down: bfloat16 [32, 768, 2560], P('expert', 'tensor'), may hold values from -0.21875 to 0.21875
- shared_gate: bfloat16 [2560, 2048], P(None, ('dp', 'tensor')), may hold values from -0.125 to 0.125
- shared_up: bfloat16 [2560, 2048], P(None, ('dp', 'tensor')), may hold values from -0.125 to 0.125
- shared_down: bfloat16 [2048, 2560], P(('dp', 'tensor')), may hold values from -0.125 to 0.125
Outputs:
- mixed: bfloat16 [2048, 2560], P(('dp', 'expert'), 'tensor')
Inputs may be any that keep to these rules, and one draw needn't show every extreme that they name: `expert_ids`: each row names 6 different experts. In each aligned block of 128 rows (the rows of one index of dp+expert) no expert is named by more than 48 rows, a bound that some blocks reach.
All inputs are finite; a program needn't handle non-finite values.
Results may differ from a plain program's by a relative error of at most 0.011.
Values may be sent and summed in bfloat16 or wider, within the bound.
A program may use at most 128 MiB of HBM per device.

v0:
```python
import jax
import jax.numpy as jnp
from jax import lax
from jax.sharding import PartitionSpec as P

D = 2560
EXPERTS = 32
TOP = 6
CAP = 48


EPSILON = 1e-06


def normalize(tokens, norm_gain):
    values = tokens.astype(jnp.float32)
    inverse = lax.rsqrt(jnp.mean(values * values, axis=1, keepdims=True) + EPSILON)
    return (values * inverse * norm_gain[None, :]).astype(jnp.bfloat16)


def slot_positions(expert_ids):
    flat_ids = expert_ids.reshape(-1)
    onehot = (flat_ids[:, None] == jnp.arange(EXPERTS, dtype=jnp.int32)[None, :]).astype(jnp.int32)
    earlier = jnp.cumsum(onehot, axis=0) - onehot
    return flat_ids * CAP + jnp.sum(earlier * onehot, axis=1)


def on_device(
    tokens,
    norm_gain,
    expert_ids,
    route_weights,
    w_gate,
    w_up,
    w_down,
    shared_gate,
    shared_up,
    shared_down,
):
    normed = normalize(tokens, norm_gain)
    tok_rows = normed.shape[0]
    tensor_count = lax.axis_size("tensor")
    half_width = D // tensor_count
    tensor_rank = lax.axis_index("tensor")
    owners = lax.axis_size("expert")
    exp_local = w_gate.shape[0]
    position = slot_positions(expert_ids)
    pair_count = position.shape[0]
    pair_token = jnp.arange(pair_count, dtype=jnp.int32) // TOP
    filler = jnp.full((EXPERTS * CAP,), -1, jnp.int32).at[position].set(pair_token)
    filled = filler >= 0
    safe_rows = jnp.maximum(filler, 0)
    source_rows = lax.dynamic_slice_in_dim(normed, tensor_rank * half_width, half_width, 1)
    outgoing = jnp.where(filled[:, None], source_rows[safe_rows], jnp.zeros((), jnp.bfloat16))
    outgoing = outgoing.reshape(EXPERTS, CAP, source_rows.shape[1])
    arrived = lax.all_to_all(outgoing, "expert", split_axis=0, concat_axis=0, tiled=True)
    arrived = lax.all_gather(arrived, "tensor", axis=2, tiled=True)
    slot_count = arrived.shape[1]
    grouped = arrived.reshape(owners, exp_local, slot_count, D)
    gate_value = jnp.einsum("jecd,edf->jecf", grouped, w_gate, preferred_element_type=jnp.float32)
    up_value = jnp.einsum("jecd,edf->jecf", grouped, w_up, preferred_element_type=jnp.float32)
    hidden = (jax.nn.silu(gate_value) * up_value).astype(jnp.bfloat16)
    partial_out = jnp.einsum("jecf,efd->jecd", hidden, w_down, preferred_element_type=jnp.float32)
    summed = lax.psum_scatter(partial_out, "tensor", scatter_dimension=3, tiled=True).astype(
        jnp.bfloat16
    )
    summed = summed.reshape(owners * exp_local, slot_count, half_width)
    result_rows = lax.all_to_all(summed, "expert", split_axis=0, concat_axis=0, tiled=True)
    piece_rows = lax.all_gather(normed, "dp", axis=0, tiled=True)
    gate_value = jnp.dot(piece_rows, shared_gate, preferred_element_type=jnp.float32)
    up_value = jnp.dot(piece_rows, shared_up, preferred_element_type=jnp.float32)
    shared_hidden = (jax.nn.silu(gate_value) * up_value).astype(jnp.bfloat16)
    start_row = jnp.int32(0)
    pieces = []
    for offset in range(tok_rows * lax.axis_size(("dp", "tensor")) // tok_rows):
        block_index = start_row // tok_rows + offset
        group_index = block_index // tensor_count
        column_index = block_index % tensor_count
        hidden_block = lax.dynamic_slice_in_dim(shared_hidden, group_index * tok_rows, tok_rows, 0)
        down_block = lax.dynamic_slice_in_dim(shared_down, column_index * half_width, half_width, 1)
        pieces.append(jnp.dot(hidden_block, down_block, preferred_element_type=jnp.float32))
    shared_part = lax.psum_scatter(
        jnp.concatenate(pieces, axis=0), ("dp", "tensor"), scatter_dimension=0, tiled=True
    )
    table = result_rows.reshape(EXPERTS * CAP, half_width)
    picked = table[position].reshape(tok_rows, TOP, half_width).astype(jnp.float32)
    scales = route_weights.astype(jnp.float32) / 64.0
    routed = jnp.sum(scales[:, :, None] * picked, axis=1)
    return (shared_part + routed).astype(jnp.bfloat16)


def solution(mesh):
    placed = (
        P(("dp", "expert"), None),
        P(),
        P(("dp", "expert"), None),
        P(("dp", "expert"), None),
        P("expert", None, "tensor"),
        P("expert", None, "tensor"),
        P("expert", "tensor", None),
        P(None, ("dp", "tensor")),
        P(None, ("dp", "tensor")),
        P(("dp", "tensor"), None),
    )
    return jax.shard_map(
        on_device,
        mesh=mesh,
        in_specs=placed,
        out_specs=P(("dp", "expert"), "tensor"),
        check_vma=False,
    )
```

profile of v0, /device:TPU:0, one launch (start us, length us, event | category | flops | bytes accessed | tf_op | source)
XLA Modules:
  0.0 326.1 jit_solution(17779378881200116879)
XLA Ops:
  8.4 1.7 reduce-window.6
  10.9 3.4 %scatter_custom_fusion = s32[1536]{0:T(1024)S(1)} fusion(s32[768]{0:T(1024)S(1)} %fusion.48, s32[768]{0:T(1024)S(1)} %add_select_fusion, s32[]{:T(128)} %constant.415.clone.1), kind=kCustom, calls=%fused_computation.73 | custom fusion | bytes 6148 | tf_op jit(solution)/shard_map/scatter | solution.py:50
  14.3 1.3 fusion.19
  15.7 1.3 fusion.21
  17.1 6.0 %gather_fusion = bf16[1536,1280]{1,0:T(8,128)(2,1)} fusion(bf16[128,1280]{1,0:T(8,128)(2,1)S(1)} %constant_dynamic-slice_fusion, s32[2048]{0:T(1024)S(1)} %pad_clamp_fusion), kind=kCustom, calls=%fused_computation | custom fusion | bytes 7870464 | tf_op jit(solution)/shard_map/gather | solution.py:54
  23.1 2.4 broadcast_select_fusion
  25.5 93.8 %all_to_all.10 = bf16[32,48,1280]{2,1,0:T(8,128)(2,1)} all-to-all(bf16[32,48,1280]{2,1,0:T(8,128)(2,1)S(1)} %broadcast_select_fusion), channel_id=1, replica_groups=mesh['dp'=4,'expert'=4,'tensor'=2] {'expert'}, dimensions={0} | all-to-all | bytes 7864320 | tf_op jit(solution)/shard_map/all_to_all | solution.py:56
  120.3 17.6 %all-gather.5.cloned.1.call-done = bf16[32,48,2560]{2,1,0:T(8,128)(2,1)} async-done(((bf16[32,48,1280]{2,1,0:T(8,128)(2,1)}), bf16[32,48,2560]{2,1,0:T(8,128)(2,1)}) %all-gather.5.cloned.1.call-update) | async-done | bytes 7864336 | tf_op jit(solution)/shard_map/all_gather | solution.py:57
  137.9 12.0 %fusion.4 = f32[8,4,48,384]{3,2,1,0:T(8,128)S(1)} fusion(bf16[8,2560,384]{2,1,0:T(8,128)(2,1)} %param.14, bf16[4,8,48,2560]{3,2,1,0:T(8,128)(2,1)} %bitcast.70), kind=kOutput, calls=%fused_computation.7 | convolution fusion | flops 3019898880 | bytes 25952256 | tf_op jit(solution)/shard_map/jecd,edf->jecf/dot_general | solution.py:60
  149.9 12.1 %fusion.11 = bf16[4,8,48,384]{3,2,0,1:T(8,128)(2,1)S(1)} fusion(f32[8,4,48,384]{3,2,1,0:T(8,128)S(1)} %fusion.4, bf16[8,2560,384]{2,1,0:T(8,128)(2,1)} %param.15, bf16[4,8,48,2560]{3,2,1,0:T(8,128)(2,1)} %bitcast.71), kind=kOutput, calls=%fused_computation.23 | convolution fusion | flops 3023437824 | bytes 27131904 | tf_op jit(solution)/shard_map/jecd,edf->jecf/dot_general | solution.py:61
  161.9 15.1 %fusion.6 = f32[4,8,48,2560]{3,2,0,1:T(8,128)} fusion(bf16[4,8,48,384]{3,2,0,1:T(8,128)(2,1)S(1)} %fusion.11, bf16[8,384,2560]{2,1,0:T(8,128)(2,1)} %param.16), kind=kOutput, calls=%fused_computation.9 | convolution fusion | flops 3019898880 | bytes 32636928 | tf_op jit(solution)/shard_map/jecf,efd->jecd/dot_general | solution.py:63
  177.3 3.1 all-gather.3.cloned.1.call-done
  180.4 2.7 fusion.49
  183.2 2.3 fusion.22
  188.8 1.2 convolution_dynamic-update-slice_fusion.4
  194.4 10.1 %reduce-scatter.5.cloned.1.call-done = f32[4,8,48,1280]{3,2,0,1:T(8,128)} async-done(((f32[4,8,48,2560]{3,2,0,1:T(8,128)}), f32[4,8,48,1280]{3,2,0,1:T(8,128)}) %reduce-scatter.5.cloned.1.call-update) | async-done | bytes 7864336 | tf_op jit(solution)/shard_map/reduce_scatter | solution.py:64
  204.5 3.6 %convert_element_type.41 = bf16[4,8,48,1280]{3,2,0,1:T(8,128)(2,1)S(1)} convert(f32[4,8,48,1280]{3,2,0,1:T(8,128)} %reduce-scatter.5.cloned.1.call-done) | non-fusion elementwise | flops 1966080 | bytes 11796480 | tf_op jit(solution)/shard_map/convert_element_type | solution.py:64
  208.1 2.2 copy.18
  210.4 5.1 %all-to-all-start.1 = ((bf16[32,48,1280]{2,1,0:T(8,128)(2,1)}), bf16[32,48,1280]{2,1,0:T(8,128)(2,1)}, u32[]{:S(2)}, u32[]{:S(2)}) async-start(bf16[32,48,1280]{2,1,0:T(8,128)(2,1)} %bitcast.68), calls=%async_computation.3 | async-start | bytes 7864320 | tf_op jit(solution)/shard_map/all_to_all | solution.py:68
  215.6 88.0 %all-to-all-done.1 = bf16[32,48,1280]{2,1,0:T(8,128)(2,1)} async-done(((bf16[32,48,1280]{2,1,0:T(8,128)(2,1)}), bf16[32,48,1280]{2,1,0:T(8,128)(2,1)}, u32[]{:S(2)}, u32[]{:S(2)}) %all-to-all-start.1) | async-done | bytes 3932192 | tf_op jit(solution)/shard_map/all_to_all | solution.py:68
  303.7 7.0 %gather_fusion.1 = bf16[768,1280]{1,0:T(8,128)(2,1)S(1)} fusion(bf16[1536,1280]{1,0:T(8,128)(2,1)} %bitcast.13, s32[1024]{0:T(1024)S(1)} %pad_clamp_fusion.1), kind=kCustom, calls=%fused_computation.1 | custom fusion | bytes 3935232 | tf_op jit(solution)/shard_map/gather | solution.py:86
  310.7 2.9 reshape.80
  313.6 4.1 %multiply_reduce_fusion = f32[128,1280]{1,0:T(8,128)S(1)} fusion(f32[128,6,1280]{2,1,0:T(8,128)} %reshape.80, f32[128,6]{1,0:T(8,128)S(1)} %copy.12), kind=kLoop, calls=%fused_computation.12 | loop fusion | flops 1802240 | bytes 4590592 | tf_op jit(solution)/shard_map/reduce_sum | solution.py:88
  317.7 1.9 add_convert_fusion
  (47 shorter events, 11.8 us)
Async XLA Ops:
  6.5 173.9 %copy-start = (bf16[2560,256]{1,0:T(8,128)(2,1)S(1)}, bf16[2560,256]{1,0:T(8,128)(2,1)}, u32[]{:S(2)}) copy-start(bf16[2560,256]{1,0:T(8,128)(2,1)} %param.17) | copy-start | bytes 3932164
  6.5 131.3 %all-gather.5.cloned.1.call-start = ((), (), s32[]{:S(2)}) async-start(), calls=%async_computation.6 | async-start | bytes 11796480 | tf_op jit(solution)/shard_map/all_gather | solution.py:57
  17.0 6.1 %copy-start.2 = (bf16[128,2560]{1,0:T(8,128)(2,1)}, bf16[128,2560]{1,0:T(8,128)(2,1)S(1)}, u32[]{:S(2)}) copy-start(bf16[128,2560]{1,0:T(8,128)(2,1)S(1)} %fusion.21) | copy-start | bytes 1966084
  119.3 61.2 %all-gather.3.cloned.1.call-start = ((), (), s32[]{:S(2)}) async-start(), calls=%async_computation.4 | async-start | bytes 3276800 | tf_op jit(solution)/shard_map/all_gather | solution.py:69
  120.0 84.5 %reduce-scatter.5.cloned.1.call-start = ((), (), s32[]{:S(2)}) async-start(), calls=%async_computation.7 | async-start | bytes 23592960 | tf_op jit(solution)/shard_map/reduce_scatter | solution.py:64
  177.1 140.6 %reduce-scatter.3.cloned.1.call-start = ((), (), s32[]{:S(2)}) async-start(), calls=%async_computation.5 | async-start | bytes 5898240 | tf_op jit(solution)/shard_map/reduce_scatter | solution.py:82
  180.4 2.7 copy-start.4
  183.2 2.3 copy-start.1
  210.4 5.1 %copy-start.3 = (s32[128,6]{0,1:T(8,128)S(1)}, s32[128,6]{0,1:T(8,128)}, u32[]{:S(2)}) copy-start(s32[128,6]{0,1:T(8,128)} %param.13) | copy-start | bytes 9220
  210.4 93.3 %all-to-all-start.1 = ((bf16[32,48,1280]{2,1,0:T(8,128)(2,1)}), bf16[32,48,1280]{2,1,0:T(8,128)(2,1)}, u32[]{:S(2)}, u32[]{:S(2)}) async-start(bf16[32,48,1280]{2,1,0:T(8,128)(2,1)} %bitcast.68), calls=%async_computation.3 | async-start | bytes 7864320 | tf_op jit(solution)/shard_map/all_to_all | solution.py:68
Sparse Core Ops, SparseCore 0:
  119.4 18.4 all-gather.4
  139.7 40.6 all-gather.2
  182.7 21.7 reduce-scatter.4
  207.7 57.7 reduce-scatter.2
where the time goes:
time: 327 us; the launch traced here: 326 us
  waiting for transfers between devices  120 us (37%)
  blocking collectives  93.8 us (29%)
  matrix products  53 us (16%)
  local copies, waits for them, and re-layouts  23.5 us (7%)
  other arithmetic  17.2 us (5%)
  between operations  13.3 us (4%)
  starting transfers between devices  5.65 us (2%)
    all_to_all x1, blocking collectives, on_device(): lax.all_to_all(outgoing, 'expert', split_axis=0, concat_axis=0, tiled=True)  93.8 us
    all_to_all x1, waiting for transfers between devices, on_device(): lax.all_to_all(summed, 'expert', split_axis=0, concat_axis=0, tiled=True)  88 us
    all_gather x1, waiting for transfers between devices, on_device(): arrived = lax.all_gather(arrived, 'tensor', axis=2, tiled=True)  17.6 us
    dot_general x1, matrix products, on_device(): jnp.einsum('jecf,efd->jecd', hidden, w_down, preferred_element_type=jnp.f...  15.1 us
    dot_general x1, matrix products, on_device(): jnp.einsum('jecd,edf->jecf', grouped, w_up, preferred_element_type=jnp.fl...  12.1 us
    dot_general x1, matrix products, on_device(): jnp.einsum('jecd,edf->jecf', grouped, w_gate, preferred_element_type=jnp....  12 us
    reduce_scatter x1, waiting for transfers between devices, on_device(): lax.psum_scatter(partial_out, 'tensor', scatter_dimension=3, tiled=True)  10.1 us
    dot_general x8, matrix products, on_device(): jnp.dot(hidden_block, down_block, preferred_element_type=jnp.float32)  8.88 us
  transfers between devices with their start and end apart: 5, of which 4 were waited for; matrix products, arithmetic and copies ran while one was open for 22% of the time, Pallas kernels for 0%

commit v1 on v0

v1 whole, which is shorter than its diff:
```python
import jax
import jax.numpy as jnp
from jax import lax
from jax.sharding import PartitionSpec as P

EPSILON = 1e-06
LANES = 128


def normalize(tokens, norm_gain):
    values = tokens.astype(jnp.float32)
    inverse = lax.rsqrt(jnp.mean(values * values, axis=1, keepdims=True) + EPSILON)
    return (values * inverse * norm_gain[None, :]).astype(jnp.bfloat16)


def by_owner(partial, blocks, width):
    rows = partial.shape[0] // blocks
    parts = partial.shape[1] // width
    split = partial.reshape(blocks, rows, parts, width)
    return split.transpose(0, 2, 1, 3).reshape(blocks * parts * rows, width)


def on_device(
    tokens,
    norm_gain,
    expert_ids,
    route_weights,
    w_gate,
    w_up,
    w_down,
    shared_gate,
    shared_up,
    shared_down,
):
    normed = normalize(tokens, norm_gain)
    rows, width = normed.shape
    owners = lax.axis_size("expert")
    groups = lax.axis_size("dp")
    half = width // lax.axis_size("tensor")
    local = w_gate.shape[0]
    experts = local * owners
    lanes = -(-experts // LANES) * LANES
    match = expert_ids[:, :, None] == jnp.arange(lanes, dtype=jnp.int32)[None, None, :]
    scale = jnp.sum(jnp.where(match, route_weights[:, :, None], 0), axis=1)
    scale = (scale.astype(jnp.float32) / 64.0).astype(jnp.bfloat16)
    sent = jnp.concatenate([normed, scale], axis=1)
    everyone = lax.all_gather(sent, "expert", axis=0, tiled=True)
    routed_rows = everyone[:, :width]
    first = lax.axis_index("expert") * local
    mine = lax.dynamic_slice_in_dim(everyone[:, width:], first, local, 1).astype(jnp.float32)
    hidden = []
    for e in range(local):
        gate = jnp.dot(routed_rows, w_gate[e], preferred_element_type=jnp.float32)
        up = jnp.dot(routed_rows, w_up[e], preferred_element_type=jnp.float32)
        hidden.append((jax.nn.silu(gate) * up * mine[:, e : e + 1]).astype(jnp.bfloat16))
    hidden = jnp.concatenate(hidden, axis=1)
    routed = jnp.dot(hidden, w_down.reshape(-1, width), preferred_element_type=jnp.float32)
    routed = by_owner(routed.astype(jnp.bfloat16), owners, half)
    routed = lax.psum_scatter(routed, ("expert", "tensor"), scatter_dimension=0, tiled=True)

    piece = lax.all_gather(normed, "dp", axis=0, tiled=True)
    gate = jnp.dot(piece, shared_gate, preferred_element_type=jnp.float32)
    up = jnp.dot(piece, shared_up, preferred_element_type=jnp.float32)
    shared = (jax.nn.silu(gate) * up).astype(jnp.bfloat16)
    shared = jnp.dot(shared, shared_down, preferred_element_type=jnp.float32)
    shared = by_owner(shared.astype(jnp.bfloat16), groups, half)
    shared = lax.psum_scatter(shared, ("dp", "tensor"), scatter_dimension=0, tiled=True)
    return (shared.astype(jnp.float32) + routed.astype(jnp.float32)).astype(jnp.bfloat16)


def solution(mesh):
    placed = (
        P(("dp", "expert"), None),
        P(),
        P(("dp", "expert"), None),
        P(("dp", "expert"), None),
        P("expert", None, "tensor"),
        P("expert", None, "tensor"),
        P("expert", "tensor", None),
        P(None, ("dp", "tensor")),
        P(None, ("dp", "tensor")),
        P(("dp", "tensor"), None),
    )
    return jax.shard_map(
        on_device,
        mesh=mesh,
        in_specs=placed,
        out_specs=P(("dp", "expert"), "tensor"),
        check_vma=False,
    )
```

time: 327 us -> 212 us (0.65)
  blocking collectives: 93.8 us -> 0 us
  other arithmetic: 17.2 us -> 7.95 us
  local copies, waits for them, and re-layouts: 23.5 us -> 17.9 us
  starting transfers between devices: 5.65 us -> 0.34 us
    all_to_all x1 -> x0, blocking collectives: 93.8 us -> none  [on_device(): lax.all_to_all(outgoing, 'expert', split_axis=0, concat_axis=0, tiled=True)]
    all_to_all x1 -> x0, waiting for transfers between devices: 88 us -> none  [on_device(): lax.all_to_all(summed, 'expert', split_axis=0, concat_axis=0, tiled=True)]
    all_gather x2, waiting for transfers between devices: 20.7 us -> 81.8 us  [the longest x1 41.9 us: on_device(): everyone = lax.all_gather(sent, 'expert', axis=0, tiled=True)]
    reduce_scatter x2, waiting for transfers between devices: 10.1 us -> 36.8 us  [the longest x1 36.8 us: on_device(): lax.psum_scatter(routed, ('expert', 'tensor'), scatter_dimension=0, tiled...]
    gather x2 -> x0, local copies, waits for them, and re-layouts: 13.1 us -> none  [the longest x1 7.02 us: on_device(): table[position].reshape(tok_rows, TOP, half_width).astype(jnp.float32)]
    reshape x0 -> x2, local copies, waits for them, and re-layouts: none -> 7.73 us  [by_owner(): split = partial.reshape(blocks, rows, parts, width)]
    transpose x0 -> x2, local copies, waits for them, and re-layouts: none -> 5.54 us  [by_owner(): return split.transpose(0, 2, 1, 3).reshape(blocks * parts * rows, width)]
    all_to_all x1 -> x0, starting transfers between devices: 5.12 us -> none  [on_device(): lax.all_to_all(summed, 'expert', split_axis=0, concat_axis=0, tiled=True)]
  transfers between devices with their start and end apart: 5 -> 4, of which waited for: 4 -> 3; matrix products, arithmetic and copies ran while one was open for 22% -> 34% of each run, Pallas kernels for 0% -> 0%
where the time goes in v1:
time: 212 us
  waiting for transfers between devices  119 us (56%)
  matrix products  53.8 us (25%)
  local copies, waits for them, and re-layouts  17.9 us (8%)
  between operations  13.4 us (6%)
  other arithmetic  7.95 us (4%)
    all_gather x1, waiting for transfers between devices, on_device(): everyone = lax.all_gather(sent, 'expert', axis=0, tiled=True)  41.9 us
    all_gather x1, waiting for transfers between devices, on_device(): piece = lax.all_gather(normed, 'dp', axis=0, tiled=True)  39.9 us
    reduce_scatter x1, waiting for transfers between devices, on_device(): lax.psum_scatter(routed, ('expert', 'tensor'), scatter_dimension=0, tiled...  36.8 us
    dot_general x8, matrix products, on_device(): up = jnp.dot(routed_rows, w_up[e], preferred_element_type=jnp.float32)  16.7 us
    dot_general x8, matrix products, on_device(): gate = jnp.dot(routed_rows, w_gate[e], preferred_element_type=jnp.float32)  15.1 us
    dot_general x1, matrix products, on_device(): jnp.dot(hidden, w_down.reshape(-1, width), preferred_element_type=jnp.flo...  13 us
    reshape x2, local copies, waits for them, and re-layouts, by_owner(): split = partial.reshape(blocks, rows, parts, width)  7.73 us
    dot_general x1, matrix products, on_device(): shared = jnp.dot(shared, shared_down, preferred_element_type=jnp.float32)  6.44 us
  transfers between devices with their start and end apart: 4, of which 3 were waited for; matrix products, arithmetic and copies ran while one was open for 34% of the time, Pallas kernels for 0%

profile of v1, /device:TPU:0, one launch (start us, length us, event | category | flops | bytes accessed | tf_op | source)
XLA Modules:
  0.0 212.0 jit_solution(12565851142378850598)
XLA Ops:
  8.0 2.2 %fusion.50 = bf16[128,2560]{1,0:T(8,128)(2,1)} fusion(bf16[128,2560]{1,0:T(8,128)(2,1)} %param.10, f32[2560]{0:T(1024)} %param.11, f32[128]{0:T(128)S(1)} %add_rsqrt_fusion), kind=kLoop, calls=%fused_computation.54 | loop fusion | flops 1310720 | bytes 1321472 | tf_op jit(solution)/shard_map/convert_element_type | solution.py:13
  10.6 2.1 pad_maximum_fusion
  12.7 39.9 %all-gather.3.cloned.1.call-done = bf16[512,2560]{1,0:T(8,128)(2,1)} async-done(((bf16[128,2560]{1,0:T(8,128)(2,1)}), bf16[512,2560]{1,0:T(8,128)(2,1)}) %all-gather.3.cloned.1.call-update) | async-done | bytes 2621456 | tf_op jit(solution)/shard_map/all_gather | solution.py:61
  52.6 2.6 %fusion.171 = f32[512,256]{1,0:T(8,128)S(1)} fusion(bf16[512,2560]{1,0:T(8,128)(2,1)} %all-gather.3.cloned.1.call-done, bf16[2560,256]{1,0:T(8,128)(2,1)S(1)} %copy-done.5), kind=kOutput, calls=%fused_computation.127 | convolution fusion | flops 671088640 | bytes 4456448 | tf_op jit(solution)/shard_map/dot_general | solution.py:62
  55.2 6.4 %convolution_convert_fusion.1 = bf16[512,2560]{1,0:T(8,128)(2,1)} fusion(bf16[256,2560]{1,0:T(8,128)(2,1)S(1)} %copy-done, bf16[512,2560]{1,0:T(8,128)(2,1)} %all-gather.3.cloned.1.call-done, bf16[2560,256]{1,0:T(8,128)(2,1)} %param.18, f32[512,256]{1,0:T(8,128)S(1)} %fusion.171), kind=kOutput, calls=%fused_computation.1 | convolution fusion | flops 1344274432 | bytes 8388608 | tf_op jit(solution)/shard_map/dot_general | solution.py:65
  61.7 5.5 %reshape.26 = bf16[4,128,2,1280]{3,2,1,0:T(2,128)(2,1)S(1)} reshape(bf16[512,2560]{1,0:T(8,128)(2,1)} %convolution_convert_fusion.1) | data formatting | bytes 5242880 | tf_op jit(solution)/shard_map/reshape | solution.py:19
  67.2 1.9 copy.19
  69.3 41.9 %all-gather.5.cloned.1.call-done = bf16[512,2688]{1,0:T(8,128)(2,1)} async-done(((bf16[128,2688]{1,0:T(8,128)(2,1)}), bf16[512,2688]{1,0:T(8,128)(2,1)}) %all-gather.5.cloned.1.call-update) | async-done | bytes 2752528 | tf_op jit(solution)/shard_map/all_gather | solution.py:47
  113.5 2.9 %fusion.30 = f32[512,384]{0,1:T(8,128)S(1)} fusion(bf16[8,2560,384]{2,1,0:T(8,128)(2,1)} %param.14, bf16[512,2688]{1,0:T(8,128)(2,1)S(1)} %copy-done.2), kind=kOutput, calls=%fused_computation.32 | convolution fusion | flops 1006632960 | bytes 5373952 | tf_op jit(solution)/shard_map/dot_general | solution.py:53
  116.5 2.9 %fusion.26 = f32[512,384]{0,1:T(8,128)S(1)} fusion(bf16[8,2560,384]{2,1,0:T(8,128)(2,1)} %param.14, bf16[512,2688]{1,0:T(8,128)(2,1)S(1)} %copy-done.2), kind=kOutput, calls=%fused_computation.28 | convolution fusion | flops 1006632960 | bytes 5373952 | tf_op jit(solution)/shard_map/dot_general | solution.py:53
  119.4 3.1 %fusion.22 = f32[512,384]{0,1:T(8,128)S(1)} fusion(bf16[8,2560,384]{2,1,0:T(8,128)(2,1)} %param.14, bf16[512,2688]{1,0:T(8,128)(2,1)S(1)} %copy-done.2), kind=kOutput, calls=%fused_computation.24 | convolution fusion | flops 1006632960 | bytes 5373952 | tf_op jit(solution)/shard_map/dot_general | solution.py:53
  129.9 2.0 fusion.144
  131.9 2.0 fusion.138
  134.0 2.3 %fusion.132 = bf16[512,3072]{0,1:T(8,128)(2,1)} fusion(bf16[512,3072]{0,1:T(8,128)(2,1)} %fusion.138, bf16[8,2560,384]{2,1,0:T(8,128)(2,1)S(1)} %bitcast.131, f32[512,384]{0,1:T(8,128)S(1)} %fusion.22, f32[512]{0:T(512)S(1)} %get-tuple-element.10, bf16[512,2688]{1,0:T(8,128)(2,1)S(1)} %copy-done.2), kind=kOutput, calls=%fused_computation.82 | convolution fusion | flops 1008009216 | bytes 5769216 | tf_op jit(solution)/shard_map/dot_general | solution.py:54
  136.3 2.1 fusion.126
  138.3 2.0 fusion.120
  141.6 2.1 fusion.114
  143.7 2.0 fusion.108
  145.7 2.1 fusion.102
  147.8 13.0 %convolution_convert_fusion = bf16[512,2560]{1,0:T(8,128)(2,1)S(1)} fusion(bf16[512,3072]{0,1:T(8,128)(2,1)} %fusion.102, bf16[3072,2560]{1,0:T(8,128)(2,1)} %bitcast.132), kind=kOutput, calls=%fused_computation | convolution fusion | flops 8054374400 | bytes 21495808 | tf_op jit(solution)/shard_map/dot_general | solution.py:57
  160.8 2.2 %reshape.29 = bf16[4,128,2,1280]{3,2,1,0:T(2,128)(2,1)} reshape(bf16[512,2560]{1,0:T(8,128)(2,1)S(1)} %convolution_convert_fusion) | data formatting | bytes 5242880 | tf_op jit(solution)/shard_map/reshape | solution.py:19
  163.0 3.7 %copy.20 = bf16[4,2,128,1280]{3,2,1,0:T(8,128)(2,1)} copy(bf16[4,2,128,1280]{3,1,2,0:T(2,128)(2,1)} %bitcast.127) | data formatting | bytes 5242880 | tf_op jit(solution)/shard_map/transpose | solution.py:20
  166.8 36.8 %reduce-scatter.5.cloned.1.call-done = bf16[128,1280]{1,0:T(8,128)(2,1)} async-done(((bf16[1024,1280]{1,0:T(8,128)(2,1)}), bf16[128,1280]{1,0:T(8,128)(2,1)}) %reduce-scatter.5.cloned.1.call-update) | async-done | bytes 327696 | tf_op jit(solution)/shard_map/reduce_scatter | solution.py:59
  203.6 1.9 add_convert_fusion
  (51 shorter events, 13.0 us)
Async XLA Ops:
  6.5 48.7 %copy-start = (bf16[256,2560]{1,0:T(8,128)(2,1)S(1)}, bf16[256,2560]{1,0:T(8,128)(2,1)}, u32[]{:S(2)}) copy-start(bf16[256,2560]{1,0:T(8,128)(2,1)} %param.19) | copy-start | bytes 3932164
  6.5 3.8 %copy-start.4 = (s32[128,6]{0,1:T(8,128)S(1)}, s32[128,6]{0,1:T(8,128)}, u32[]{:S(2)}) copy-start(s32[128,6]{0,1:T(8,128)} %param.12) | copy-start | bytes 9220
  6.5 3.8 %copy-start.3 = (s32[128,6]{0,1:T(8,128)S(1)}, s32[128,6]{0,1:T(8,128)}, u32[]{:S(2)}) copy-start(s32[128,6]{0,1:T(8,128)} %param.13) | copy-start | bytes 9220
  6.5 46.1 %copy-start.5 = (bf16[2560,256]{1,0:T(8,128)(2,1)S(1)}, bf16[2560,256]{1,0:T(8,128)(2,1)}, u32[]{:S(2)}) copy-start(bf16[2560,256]{1,0:T(8,128)(2,1)} %param.17) | copy-start | bytes 3932164
  6.5 46.1 %all-gather.3.cloned.1.call-start = ((), (), s32[]{:S(2)}) async-start(), calls=%async_computation.2 | async-start | bytes 3276800 | tf_op jit(solution)/shard_map/all_gather | solution.py:61
  10.3 100.9 %all-gather.5.cloned.1.call-start = ((), (), s32[]{:S(2)}) async-start(), calls=%async_computation.4 | async-start | bytes 3440640 | tf_op jit(solution)/shard_map/all_gather | solution.py:47
  12.7 154.1 %reduce-scatter.3.cloned.1.call-start = ((), (), s32[]{:S(2)}) async-start(), calls=%async_computation.3 | async-start | bytes 2949120 | tf_op jit(solution)/shard_map/reduce_scatter | solution.py:67
  69.1 134.5 %reduce-scatter.5.cloned.1.call-start = ((), (), s32[]{:S(2)}) async-start(), calls=%async_computation.5 | async-start | bytes 2949120 | tf_op jit(solution)/shard_map/reduce_scatter | solution.py:59
  111.2 2.3 %copy-start.2 = (bf16[512,2688]{1,0:T(8,128)(2,1)S(1)}, bf16[512,2688]{1,0:T(8,128)(2,1)}, u32[]{:S(2)}) copy-start(bf16[512,2688]{1,0:T(8,128)(2,1)} %all-gather.5.cloned.1.call-done) | copy-start | bytes 8257540
  113.5 9.0 %slice-start = ((s8[15728640]{0:T(1024)(128)(4,1)}), s8[4194304]{0:T(1024)(128)(4,1)S(1)}, s32[]{:S(2)}) async-start(s8[15728640]{0:T(1024)(128)(4,1)} %bitcast.128), calls=%async_computation.6 | async-start | bytes 8388608
  113.5 9.0 %slice-start.1 = ((s8[15728640]{0:T(1024)(128)(4,1)}), s8[4194304]{0:T(1024)(128)(4,1)S(1)}, s32[]{:S(2)}) async-start(s8[15728640]{0:T(1024)(128)(4,1)} %bitcast.128), calls=%async_computation.7 | async-start | bytes 8388608
  116.4 6.1 %slice-start.2 = ((s8[15728640]{0:T(1024)(128)(4,1)}), s8[4194304]{0:T(1024)(128)(4,1)S(1)}, s32[]{:S(2)}) async-start(s8[15728640]{0:T(1024)(128)(4,1)} %bitcast.128), calls=%async_computation.8 | async-start | bytes 8388608
  119.4 3.1 %slice-start.3 = ((s8[15728640]{0:T(1024)(128)(4,1)}), s8[3145728]{0:T(1024)(128)(4,1)S(1)}, s32[]{:S(2)}) async-start(s8[15728640]{0:T(1024)(128)(4,1)} %bitcast.128), calls=%async_computation.9 | async-start | bytes 6291456
  123.8 3.8 %slice-start.4 = ((s8[15728640]{0:T(1024)(128)(4,1)}), s8[4194304]{0:T(1024)(128)(4,1)S(1)}, s32[]{:S(2)}) async-start(s8[15728640]{0:T(1024)(128)(4,1)} %bitcast.130), calls=%async_computation.10 | async-start | bytes 8388608
  123.8 3.8 %slice-start.5 = ((s8[15728640]{0:T(1024)(128)(4,1)}), s8[4194304]{0:T(1024)(128)(4,1)S(1)}, s32[]{:S(2)}) async-start(s8[15728640]{0:T(1024)(128)(4,1)} %bitcast.130), calls=%async_computation.11 | async-start | bytes 8388608
  125.0 4.0 %slice-start.6 = ((s8[15728640]{0:T(1024)(128)(4,1)}), s8[4194304]{0:T(1024)(128)(4,1)S(1)}, s32[]{:S(2)}) async-start(s8[15728640]{0:T(1024)(128)(4,1)} %bitcast.130), calls=%async_computation.12 | async-start | bytes 8388608
  126.3 3.6 %slice-start.7 = ((s8[15728640]{0:T(1024)(128)(4,1)}), s8[3145728]{0:T(1024)(128)(4,1)S(1)}, s32[]{:S(2)}) async-start(s8[15728640]{0:T(1024)(128)(4,1)} %bitcast.130), calls=%async_computation.13 | async-start | bytes 6291456
  163.0 42.4 %copy-start.1 = (bf16[256,2560]{1,0:T(8,128)(2,1)S(1)}, bf16[256,2560]{1,0:T(8,128)(2,1)}, u32[]{:S(2)}) copy-start(bf16[256,2560]{1,0:T(8,128)(2,1)} %param.19) | copy-start | bytes 3932164
Sparse Core Ops, SparseCore 0:
  10.4 42.2 all-gather.2
  54.2 56.9 all-gather.4
  114.5 42.2 reduce-scatter.2
  166.8 36.6 reduce-scatter.4

commit v2 on v1

v2 whole, which is shorter than its diff:
```python
import functools

import jax
import jax.numpy as jnp
from jax import lax
from jax.experimental import pallas as pl
from jax.experimental.pallas import tpu as pltpu
from jax.sharding import PartitionSpec as P

EPSILON = 1e-06
LANES = 128
MESH = pl.DeviceIdType.MESH
VMEM_BYTES = 67043328


def dot(a, b):
    return jnp.dot(a, b, preferred_element_type=jnp.float32)


def kernel(
    owners,
    groups,
    tokens,
    gain,
    ids,
    weights,
    w_gate,
    w_up,
    w_down,
    shared_gate,
    shared_up,
    shared_down,
    out,
    blocks,
    peers,
    gate_up,
    down,
    shared_in,
    shared_out,
    hidden,
    shared_hidden,
    staged,
    keep,
    total,
    partner_routed,
    partner_shared,
    landed,
    load_sem,
    shared_sem,
    token_sem,
    zsend,
    zrecv,
    gsend,
    grecv,
    fsend,
    frecv,
    esend,
    erecv,
    rsend,
    rrecv,
):
    g = lax.axis_index("dp")
    z = lax.axis_index("expert")
    c = lax.axis_index("tensor")
    other = 1 - c
    local, ff, width = w_down.shape
    sff = shared_down.shape[0]
    rows = tokens.shape[0]
    half = width // 2
    lanes = blocks.shape[2] - width
    my_rows = pl.ds(pl.multiple_of(c * (rows // 2), rows // 2), rows // 2)
    its_rows = pl.ds(pl.multiple_of(other * (rows // 2), rows // 2), rows // 2)

    token_loads = [
        pltpu.make_async_copy(tokens.at[:, pl.ds(p * half, half)], staged.at[p], token_sem.at[p])
        for p in range(2)
    ]
    for load in token_loads:
        load.start()

    def expert_loads(e):
        first = pl.ds(pl.multiple_of(e * ff, LANES), ff)
        return (
            pltpu.make_async_copy(w_gate.at[e], gate_up.at[e, :, pl.ds(0, ff)], load_sem.at[0, e]),
            pltpu.make_async_copy(w_up.at[e], gate_up.at[e, :, pl.ds(ff, ff)], load_sem.at[1, e]),
            pltpu.make_async_copy(w_down.at[e], down.at[first], load_sem.at[2, e]),
        )

    shared_loads = (
        pltpu.make_async_copy(shared_gate, shared_in.at[:, pl.ds(0, sff)], shared_sem.at[0]),
        pltpu.make_async_copy(shared_up, shared_in.at[:, pl.ds(sff, sff)], shared_sem.at[1]),
        pltpu.make_async_copy(shared_down, shared_out, shared_sem.at[2]),
    )
    for e in range(local):
        expert_loads(e)[0].start()
        expert_loads(e)[1].start()
    for e in range(local):
        expert_loads(e)[2].start()
    for load in shared_loads:
        load.start()

    barrier = pltpu.get_barrier_semaphore()
    for r in range(1, owners):
        peer = {"expert": lax.rem(z + r, owners)}
        pl.semaphore_signal(barrier, inc=1, device_id=peer, device_id_type=MESH)
    for r in range(1, groups):
        peer = {"dp": lax.rem(g + r, groups)}
        pl.semaphore_signal(barrier, inc=1, device_id=peer, device_id_type=MESH)
    pl.semaphore_signal(barrier, inc=1, device_id={"tensor": other}, device_id_type=MESH)

    for load in token_loads:
        load.wait()
    step = 16

    def norm(t, carry):
        span = pl.ds(pl.multiple_of(t * step, step), step)
        left = staged[0, span, :].astype(jnp.float32)
        right = staged[1, span, :].astype(jnp.float32)
        square = jnp.sum(left * left, axis=1, keepdims=True)
        square = square + jnp.sum(right * right, axis=1, keepdims=True)
        inverse = lax.rsqrt(square / width + EPSILON)
        blocks[z, span, 0:half] = (left * inverse * gain[:, 0:half]).astype(jnp.bfloat16)
        blocks[z, span, half:width] = (right * inverse * gain[:, half:width]).astype(jnp.bfloat16)
        lane = lax.broadcasted_iota(jnp.int32, (step, lanes), 1)
        scale = jnp.zeros((step, lanes), jnp.float32)
        for k in range(ids.shape[1]):
            weight = weights[span, k : k + 1].astype(jnp.float32) / 64.0
            scale = scale + jnp.where(ids[span, k : k + 1] == lane, weight, 0.0)
        blocks[z, span, width : width + lanes] = scale.astype(jnp.bfloat16)
        return carry

    lax.fori_loop(0, rows // step, norm, 0)

    pl.semaphore_wait(barrier, owners + groups - 1)

    def block_send(r):
        return pltpu.make_async_remote_copy(
            src_ref=blocks.at[z, my_rows],
            dst_ref=blocks.at[z, my_rows],
            send_sem=zsend.at[r - 1],
            recv_sem=zrecv.at[z],
            device_id={"expert": lax.rem(z + r, owners)},
            device_id_type=MESH,
        )

    def peer_send(r):
        return pltpu.make_async_remote_copy(
            src_ref=blocks.at[z, my_rows, pl.ds(0, width)],
            dst_ref=peers.at[r - 1, my_rows],
            send_sem=gsend.at[r - 1],
            recv_sem=grecv.at[r - 1],
            device_id={"dp": lax.rem(g + r, groups)},
            device_id_type=MESH,
        )

    for r in sorted(range(1, owners), key=lambda r: min(r, owners - r)):
        block_send(r).start()
    for r in range(1, groups):
        peer_send(r).start()

    def pass_on(ref, span, index):
        return pltpu.make_async_remote_copy(
            src_ref=ref.at[span],
            dst_ref=ref.at[span],
            send_sem=fsend.at[index],
            recv_sem=frecv.at[index],
            device_id={"tensor": other},
            device_id_type=MESH,
        )

    def exchange(slot, where, index):
        return pltpu.make_async_remote_copy(
            src_ref=staged.at[slot],
            dst_ref=where,
            send_sem=esend.at[index],
            recv_sem=erecv.at[index],
            device_id={"tensor": other},
            device_id_type=MESH,
        )

    def result_send(src, slot, device):
        return pltpu.make_async_remote_copy(
            src_ref=src,
            dst_ref=landed.at[slot],
            send_sem=rsend.at[slot],
            recv_sem=rrecv.at[slot],
            device_id=device,
            device_id_type=MESH,
        )

    upper = z >= owners // 2
    near = jnp.where(upper, owners - 1 - z, z)

    def source(i):
        walk = jnp.where(i > near, i, near - i)
        return jnp.where(upper, owners - 1 - walk, walk)

    def fetch(i):
        b = source(i)
        pltpu.make_async_copy(blocks.at[b, my_rows], blocks.at[b, my_rows], zrecv.at[b]).wait()
        pass_on(blocks.at[b], my_rows, b).start()

    chunk = 256
    spans = half // chunk

    def routed(i, own):
        b = source(i)
        if not own:
            pass_on(blocks.at[b], its_rows, b).wait_recv()
        first = z * local

        def expert(e, carry):
            if own:
                expert_loads(e)[0].wait()
                expert_loads(e)[1].wait()
            both = dot(blocks[b, :, 0:width], gate_up[e])
            gate = both[:, 0:ff]
            lane = lax.broadcasted_iota(jnp.int32, (rows, lanes), 1)
            scale = blocks[b, :, width : width + lanes].astype(jnp.float32)
            scale = jnp.sum(jnp.where(lane == first + e, scale, 0.0), axis=1, keepdims=True)
            value = gate / (1.0 + jnp.exp(-gate)) * both[:, ff:] * scale
            hidden[:, pl.ds(pl.multiple_of(e * ff, LANES), ff)] = value.astype(jnp.bfloat16)
            return carry

        lax.fori_loop(0, local, expert, 0)
        if own:
            fetch(1)
            for e in range(local):
                expert_loads(e)[2].wait()
        else:

            @pl.when(i + 1 < owners)
            def _():
                fetch(i + 1)

        def theirs(n, carry):
            at = pl.ds(pl.multiple_of(other * half + n * chunk, LANES), chunk)
            to = pl.ds(pl.multiple_of(n * chunk, LANES), chunk)
            staged[0, :, to] = dot(hidden[...], down[:, at]).astype(jnp.bfloat16)
            return carry

        def ours(n, carry):
            at = pl.ds(pl.multiple_of(c * half + n * chunk, LANES), chunk)
            to = pl.ds(pl.multiple_of(n * chunk, LANES), chunk)
            keep[:, to] = dot(hidden[...], down[:, at])
            return carry

        lax.fori_loop(0, spans, theirs, 0)
        swap = exchange(0, partner_routed.at[i], i)
        swap.start()
        lax.fori_loop(0, spans, ours, 0)
        swap.wait()
        if own:
            total[...] = keep[...] + partner_routed[i].astype(jnp.float32)
        else:
            summed = keep[...] + partner_routed[i].astype(jnp.float32)
            partner_routed[i] = summed.astype(jnp.bfloat16)
            slot = lax.rem(z - b + owners, owners) - 1
            result_send(partner_routed.at[i], slot, {"expert": b}).start()

    def shared_first(j, block):
        both = dot(block, shared_in[...])
        gate = both[:, 0:sff]
        value = gate / (1.0 + jnp.exp(-gate)) * both[:, sff:]
        shared_hidden[j] = value.astype(jnp.bfloat16)

    routed(0, True)

    for r in range(1, groups):
        here = peers.at[r - 1, my_rows]
        pltpu.make_async_copy(here, here, grecv.at[r - 1]).wait()
        pass_on(peers.at[r - 1], my_rows, owners + r - 1).start()
    for load in shared_loads:
        load.wait()
    shared_first(0, blocks[z, :, 0:width])

    def shared_peer(j, carry):
        pass_on(peers.at[j - 1], its_rows, owners + j - 1).wait_recv()
        shared_first(j, peers[j - 1])
        return carry

    lax.fori_loop(1, groups, shared_peer, 0)

    def shared_theirs(j, carry):
        at = pl.ds(pl.multiple_of(other * half, LANES), half)
        staged[j] = dot(shared_hidden[j], shared_out[:, at]).astype(jnp.bfloat16)
        exchange(j, partner_shared.at[j], owners + j).start()
        return carry

    lax.fori_loop(0, groups, shared_theirs, 0)

    def shared_ours(j, carry):
        at = pl.ds(pl.multiple_of(c * half, LANES), half)
        keep[...] = dot(shared_hidden[j], shared_out[:, at])
        exchange(j, partner_shared.at[j], owners + j).wait()
        summed = keep[...] + partner_shared[j].astype(jnp.float32)

        @pl.when(j == 0)
        def _():
            total[...] = total[...] + summed

        @pl.when(j > 0)
        def _():
            partner_shared[j] = summed.astype(jnp.bfloat16)
            device = {"dp": lax.rem(g - j + groups, groups)}
            result_send(partner_shared.at[j], owners - 1 + j - 1, device).start()

        return carry

    lax.fori_loop(0, groups, shared_ours, 0)

    def others(i, carry):
        routed(i, False)
        return carry

    lax.fori_loop(1, owners, others, 0)

    for s in range(owners + groups - 2):
        result_send(partner_routed.at[0], s, {"tensor": other}).wait_recv()
    final = total[...]
    for s in range(owners + groups - 2):
        final = final + landed[s].astype(jnp.float32)
    staged[0] = final.astype(jnp.bfloat16)
    store = pltpu.make_async_copy(staged.at[0], out, token_sem.at[0])
    store.start()
    for r in range(1, owners):
        block_send(r).wait_send()
        b = lax.rem(z + r, owners)
        pass_on(blocks.at[b], my_rows, b).wait_send()
    for r in range(1, groups):
        peer_send(r).wait_send()
        pass_on(peers.at[r - 1], my_rows, owners + r - 1).wait_send()
    for s in range(owners + groups - 2):
        result_send(partner_routed.at[0], s, {"tensor": other}).wait_send()
    store.wait()


def on_device(owners, groups, tokens, norm_gain, expert_ids, route_weights, *matrices):
    w_gate, w_up, w_down, shared_gate, shared_up, shared_down = matrices
    rows, width = tokens.shape
    half = width // 2
    local, ff, _ = w_down.shape
    sff = shared_down.shape[0]
    lanes = -(-local * owners // LANES) * LANES
    bf16, f32 = jnp.bfloat16, jnp.float32
    dma = pltpu.SemaphoreType.DMA
    vmem = pl.BlockSpec(memory_space=pltpu.VMEM)
    anywhere = pl.BlockSpec(memory_space=pl.ANY)
    links = owners + groups
    return pl.pallas_call(
        functools.partial(kernel, owners, groups),
        out_shape=jax.ShapeDtypeStruct((rows, half), bf16),
        in_specs=[anywhere, vmem, vmem, vmem] + [anywhere] * 6,
        out_specs=anywhere,
        scratch_shapes=[
            pltpu.VMEM((owners, rows, width + lanes), bf16),
            pltpu.VMEM((groups - 1, rows, width), bf16),
            pltpu.VMEM((local, width, 2 * ff), bf16),
            pltpu.VMEM((local * ff, width), bf16),
            pltpu.VMEM((width, 2 * sff), bf16),
            pltpu.VMEM((sff, width), bf16),
            pltpu.VMEM((rows, local * ff), bf16),
            pltpu.VMEM((groups, rows, sff), bf16),
            pltpu.VMEM((max(groups, 2), rows, half), bf16),
            pltpu.VMEM((rows, half), f32),
            pltpu.VMEM((rows, half), f32),
            pltpu.VMEM((owners, rows, half), bf16),
            pltpu.VMEM((groups, rows, half), bf16),
            pltpu.VMEM((links - 2, rows, half), bf16),
            dma((3, local)),
            dma((3,)),
            dma((2,)),
            dma((owners - 1,)),
            dma((owners,)),
            dma((groups - 1,)),
            dma((groups - 1,)),
            dma((links - 1,)),
            dma((links - 1,)),
            dma((links,)),
            dma((links,)),
            dma((links - 2,)),
            dma((links - 2,)),
        ],
        compiler_params=pltpu.CompilerParams(
            collective_id=0, has_side_effects=True, vmem_limit_bytes=VMEM_BYTES
        ),
    )(tokens, norm_gain[None, :], expert_ids, route_weights, *matrices)


def solution(mesh):
    placed = (
        P(("dp", "expert"), None),
        P(),
        P(("dp", "expert"), None),
        P(("dp", "expert"), None),
        P("expert", None, "tensor"),
        P("expert", None, "tensor"),
        P("expert", "tensor", None),
        P(None, ("dp", "tensor")),
        P(None, ("dp", "tensor")),
        P(("dp", "tensor"), None),
    )
    return jax.shard_map(
        functools.partial(on_device, mesh.shape["expert"], mesh.shape["dp"]),
        mesh=mesh,
        in_specs=placed,
        out_specs=P(("dp", "expert"), "tensor"),
        check_vma=False,
    )
```

time: 212 us -> 104 us (0.49)
  waiting for transfers between devices: 119 us -> 0 us
  Pallas kernels: 0 us -> 97.9 us
  matrix products: 53.8 us -> 0 us
  between operations: 13.4 us -> 0.01 us
  local copies, waits for them, and re-layouts: 17.9 us -> 5.87 us
  other arithmetic: 7.95 us -> 0 us
    pallas_call x0 -> x1, Pallas kernels: none -> 97.9 us  [on_device(): pl.pallas_call(functools.partial(kernel, owners, groups), out_shape=jax.S...]
    all_gather x2 -> x0, waiting for transfers between devices: 81.8 us -> none  [the longest x1 41.9 us: on_device(): everyone = lax.all_gather(sent, 'expert', axis=0, tiled=True)]
    dot_general x19 -> x0, matrix products: 53.8 us -> none  [the longest x8 16.7 us: on_device(): up = jnp.dot(routed_rows, w_up[e], preferred_element_type=jnp.float32)]
    reduce_scatter x2 -> x0, waiting for transfers between devices: 36.8 us -> none  [the longest x1 36.8 us: on_device(): lax.psum_scatter(routed, ('expert', 'tensor'), scatter_dimension=0, tiled...]
    reshape x2 -> x0, local copies, waits for them, and re-layouts: 7.73 us -> none  [by_owner(): split = partial.reshape(blocks, rows, parts, width)]
    transpose x2 -> x0, local copies, waits for them, and re-layouts: 5.54 us -> none  [by_owner(): return split.transpose(0, 2, 1, 3).reshape(blocks * parts * rows, width)]
    convert_element_type x4 -> x0, other arithmetic: 4.17 us -> none  [the longest x1 2.19 us: normalize(): return (values * inverse * norm_gain[None, :]).astype(jnp.bfloat16)]
    slice x2 -> x0, local copies, waits for them, and re-layouts: 2.19 us -> none  [the longest x1 1.12 us: on_device(): mine[:, e:e + 1]]
  transfers between devices with their start and end apart: 4 -> 0, of which waited for: 3 -> 0; matrix products, arithmetic and copies ran while one was open for 34% -> 0% of each run, Pallas kernels for 0% -> 0%
where the time goes in v2:
time: 104 us
  Pallas kernels  97.9 us (94%)
  local copies, waits for them, and re-layouts  5.87 us (6%)
    pallas_call x1, Pallas kernels, on_device(): pl.pallas_call(functools.partial(kernel, owners, groups), out_shape=jax.S...  97.9 us
    unnamed x3, local copies, waits for them, and re-layouts  4.56 us

profile of v2, /device:TPU:0, one launch (start us, length us, event | category | flops | bytes accessed | tf_op | source)
XLA Modules:
  0.0 103.7 jit_solution(7707578720240999548)
XLA Ops:
  0.0 1.3 %broadcast_in_dim.3.gain = f32[1,2560]{1,0:T(1,128)} reshape(f32[2560]{0:T(1024)} %param.11) | data formatting | bytes 20480 | tf_op jit(solution)/shard_map/broadcast_in_dim | solution.py:387
  1.3 1.4 %copy.11.ids = s32[128,6]{1,0:T(8,128)} copy(s32[128,6]{0,1:T(8,128)} %param.12) | data formatting | bytes 6144 | tf_op args[2]
  2.7 1.4 %copy.12.weights = s32[128,6]{1,0:T(8,128)} copy(s32[128,6]{0,1:T(8,128)} %param.13) | data formatting | bytes 6144 | tf_op args[3]
  4.2 97.9 %shard_map.100 = bf16[128,1280]{1,0:T(8,128)(2,1)} custom-call(bf16[128,2560]{1,0:T(8,128)(2,1)} %tokens.1, f32[1,2560]{1,0:T(1,128)} %broadcast_in_dim.3.gain, s32[128,6]{1,0:T(8,128)} %copy.11.ids, s32[128,6]{1,0:T(8,128)} %copy.12.weights, bf16[8,2560,384]{2,1,0:T(8,128)(2,1)} %w_gate.1, bf16[8,2560,384]{2,1,0:T(8,128)(2,1)} %w_up.1, ...), custom_call_target="tpu_custom_call" | custom-call | tf_op jit(solution)/shard_map/pallas_call | solution.py:350
  102.0 1.7 %copy.14 = bf16[128,1280]{1,0:T(8,128)(2,1)} copy(bf16[128,1280]{1,0:T(8,128)(2,1)} %shard_map.100) | data formatting | bytes 655360

commit v3 on v2

--- a/solution.py
+++ b/solution.py
@@ -133,13 +133,13 @@
 
     pl.semaphore_wait(barrier, owners + groups - 1)
 
-    def block_send(r):
+    def block_send(b, way):
         return pltpu.make_async_remote_copy(
-            src_ref=blocks.at[z, my_rows],
-            dst_ref=blocks.at[z, my_rows],
-            send_sem=zsend.at[r - 1],
-            recv_sem=zrecv.at[z],
-            device_id={"expert": lax.rem(z + r, owners)},
+            src_ref=blocks.at[b, my_rows],
+            dst_ref=blocks.at[b, my_rows],
+            send_sem=zsend.at[way, b],
+            recv_sem=zrecv.at[b],
+            device_id={"expert": lax.rem(z + (1 if way else owners - 1), owners)},
             device_id_type=MESH,
         )
 
@@ -153,8 +153,14 @@
             device_id_type=MESH,
         )
 
-    for r in sorted(range(1, owners), key=lambda r: min(r, owners - r)):
-        block_send(r).start()
+    @pl.when(z + 1 < owners)
+    def _():
+        block_send(z, 1).start()
+
+    @pl.when(z > 0)
+    def _():
+        block_send(z, 0).start()
+
     for r in range(1, groups):
         peer_send(r).start()
 
@@ -195,10 +201,29 @@
         walk = jnp.where(i > near, i, near - i)
         return jnp.where(upper, owners - 1 - walk, walk)
 
-    def fetch(i):
-        b = source(i)
+    def arrive(b):
         pltpu.make_async_copy(blocks.at[b, my_rows], blocks.at[b, my_rows], zrecv.at[b]).wait()
-        pass_on(blocks.at[b], my_rows, b).start()
+
+    def fetch(d):
+        @pl.when(z - d >= 0)
+        def _():
+            arrive(z - d)
+
+            @pl.when(z + 1 < owners)
+            def _():
+                block_send(z - d, 1).start()
+
+            pass_on(blocks.at[z - d], my_rows, z - d).start()
+
+        @pl.when(z + d < owners)
+        def _():
+            arrive(z + d)
+
+            @pl.when(z > 0)
+            def _():
+                block_send(z + d, 0).start()
+
+            pass_on(blocks.at[z + d], my_rows, z + d).start()
 
     chunk = 256
     spans = half // chunk
@@ -229,9 +254,9 @@
                 expert_loads(e)[2].wait()
         else:
 
-            @pl.when(i + 1 < owners)
+            @pl.when(i + 2 < owners)
             def _():
-                fetch(i + 1)
+                fetch(i + 2)
 
         def theirs(n, carry):
             at = pl.ds(pl.multiple_of(other * half + n * chunk, LANES), chunk)
@@ -288,6 +313,8 @@
         return carry
 
     lax.fori_loop(0, groups, shared_theirs, 0)
+    if owners > 2:
+        fetch(2)
 
     def shared_ours(j, carry):
         at = pl.ds(pl.multiple_of(c * half, LANES), half)
@@ -324,9 +351,18 @@
     store = pltpu.make_async_copy(staged.at[0], out, token_sem.at[0])
     store.start()
     for r in range(1, owners):
-        block_send(r).wait_send()
         b = lax.rem(z + r, owners)
         pass_on(blocks.at[b], my_rows, b).wait_send()
+    for b in range(owners):
+
+        @pl.when((b <= z) & (z + 1 < owners))
+        def _():
+            block_send(b, 1).wait_send()
+
+        @pl.when((b >= z) & (z > 0))
+        def _():
+            block_send(b, 0).wait_send()
+
     for r in range(1, groups):
         peer_send(r).wait_send()
         pass_on(peers.at[r - 1], my_rows, owners + r - 1).wait_send()
@@ -370,7 +406,7 @@
             dma((3, local)),
             dma((3,)),
             dma((2,)),
-            dma((owners - 1,)),
+            dma((2, owners)),
             dma((owners,)),
             dma((groups - 1,)),
             dma((groups - 1,)),

time: 104 us -> 99 us (0.952)
  Pallas kernels: 97.9 us -> 92.8 us
    pallas_call x1, Pallas kernels: 97.9 us -> 92.8 us  [on_device(): pl.pallas_call(functools.partial(kernel, owners, groups), out_shape=jax.S...]
where the time goes in v3:
time: 99 us; the launch traced here: 98.7 us
  Pallas kernels  92.8 us (94%)
  local copies, waits for them, and re-layouts  5.87 us (6%)
    pallas_call x1, Pallas kernels, on_device(): pl.pallas_call(functools.partial(kernel, owners, groups), out_shape=jax.S...  92.8 us
    unnamed x3, local copies, waits for them, and re-layouts  4.56 us

profile of v3, /device:TPU:0, one launch (start us, length us, event | category | flops | bytes accessed | tf_op | source)
XLA Modules:
  0.0 98.7 jit_solution(8420815450349229717)
XLA Ops:
  0.0 1.3 %broadcast_in_dim.3.gain = f32[1,2560]{1,0:T(1,128)} reshape(f32[2560]{0:T(1024)} %param.11) | data formatting | bytes 20480 | tf_op jit(solution)/shard_map/broadcast_in_dim | solution.py:423
  1.3 1.4 %copy.11.ids = s32[128,6]{1,0:T(8,128)} copy(s32[128,6]{0,1:T(8,128)} %param.12) | data formatting | bytes 6144 | tf_op args[2]
  2.7 1.4 %copy.12.weights = s32[128,6]{1,0:T(8,128)} copy(s32[128,6]{0,1:T(8,128)} %param.13) | data formatting | bytes 6144 | tf_op args[3]
  4.2 92.8 %shard_map.100 = bf16[128,1280]{1,0:T(8,128)(2,1)} custom-call(bf16[128,2560]{1,0:T(8,128)(2,1)} %tokens.1, f32[1,2560]{1,0:T(1,128)} %broadcast_in_dim.3.gain, s32[128,6]{1,0:T(8,128)} %copy.11.ids, s32[128,6]{1,0:T(8,128)} %copy.12.weights, bf16[8,2560,384]{2,1,0:T(8,128)(2,1)} %w_gate.1, bf16[8,2560,384]{2,1,0:T(8,128)(2,1)} %w_up.1, ...), custom_call_target="tpu_custom_call" | custom-call | tf_op jit(solution)/shard_map/pallas_call | solution.py:386
  97.0 1.7 %copy.14 = bf16[128,1280]{1,0:T(8,128)(2,1)} copy(bf16[128,1280]{1,0:T(8,128)(2,1)} %shard_map.100) | data formatting | bytes 655360
